TPU v7x, 32 devices: a whole 2x2x4 slice. The times are simulated.
32 devices in a mesh: row: 8 (over y, x, core), col: 4 (over z).
Axes of the slice: x: 2, y: 2, z: 4, core: 2. Of those that a mesh axis runs over, the one named last changes fastest.
Arguments:
- tile_u: float32 [8, 16, 2048, 128], P('row', 'col'), may hold values from -6 to 6
- tile_v: float32 [8, 16, 2048, 128], P('row', 'col'), may hold values from -1.5 to 1.5
- row_panel_u: float32 [8, 2048, 128], P('row', 'col'), may hold values from -6 to 6
- row_panel_v: float32 [8, 2048, 128], P('row', 'col'), may hold values from -0.125 to 0.125
- col_panel_u: float32 [16, 2048, 128], P('row', 'col'), may hold values from -6 to 6
- col_panel_v: float32 [16, 2048, 128], P('row', 'col'), may hold values from -0.125 to 0.125
- diag_inverse: float32 [2048, 2048], P('col'), may hold values from -0.15 to 2, as said below
- sketch: float32 [2048, 128], replicated, may hold values from -0.125 to 0.125
Outputs:
- new_u: float32 [8, 16, 2048, 128], P('row', 'col')
- new_v: float32 [8, 16, 2048, 128], P('row', 'col')
Inputs may be any that keep to these rules, and one draw needn't show every extreme that they name: `diag_inverse`: lower triangular; the diagonal lies between 0.5 and 2, the entries below it between -0.15 and 0.15.
All inputs are finite; a program needn't handle non-finite values.
Results may differ from a plain program's by a relative error of at most 0.0003.
Values sent between devices are 32-bit elements; how exact they have to be, the bound alone decides.
No kernel may reach another device: no remote copies, remote signals or barrier semaphores. Data moves between devices by JAX's collectives and lax.ppermute only.
A program may use at most 128 MiB of HBM per device.

v0:
```python
import math
import jax
import jax.numpy as jnp
from jax import lax
from jax.sharding import PartitionSpec as P

highest = lax.Precision.HIGHEST


def body(tile_u, tile_v, row_panel_u, row_panel_v, col_panel_u, col_panel_v, diag_inverse, sketch):
    first = jnp.einsum(
        "ab,tbk->tak",
        diag_inverse,
        lax.all_gather(row_panel_v, "col", axis=1, tiled=True),
        precision=highest,
    )
    second = jnp.einsum(
        "ab,tbk->tak",
        diag_inverse,
        lax.all_gather(col_panel_v, "col", axis=1, tiled=True),
        precision=highest,
    )
    col_u_rows, col_v_rows = (
        lax.all_gather(col_panel_u, "row", axis=0, tiled=True),
        lax.all_gather(second, "row", axis=0, tiled=True),
    )
    row_u_full = lax.all_gather(row_panel_u, "col", axis=1, tiled=True)
    col_u_full = lax.all_to_all(col_u_rows, "col", split_axis=0, concat_axis=1, tiled=True)
    partial_cores = jnp.einsum("iak,jal->ijkl", first, col_v_rows, precision=highest)
    cores = lax.psum_scatter(partial_cores, "col", scatter_dimension=1, tiled=True)
    branch = -jnp.einsum("iak,ijkl->ijal", row_u_full, cores, precision=highest)
    left_side = jnp.concatenate([tile_u, branch], axis=-1)
    right_side = jnp.concatenate([tile_v, col_u_full[None]], axis=-1)
    projected = jnp.einsum("ijar,ak->ijrk", right_side, sketch, precision=highest)
    sample = jnp.einsum("ijar,ijrk->ijak", left_side, projected, precision=highest)
    gram_matrix = jnp.einsum("ijak,ijal->ijkl", sample, sample, precision=highest)
    factor = jnp.linalg.cholesky(gram_matrix)
    solved_t = jax.scipy.linalg.solve_triangular(factor, jnp.swapaxes(sample, -1, -2), lower=True)
    basis = jnp.swapaxes(solved_t, -1, -2)
    coefficients = jnp.einsum("ijar,ijak->ijrk", left_side, basis, precision=highest)
    scaling = math.sqrt(tile_u.shape[2])
    new_v = jnp.einsum("ijar,ijrk->ijak", right_side, coefficients, precision=highest) / scaling
    return (basis * scaling, new_v)


def solution(mesh):
    in_specs = (
        P("row", "col", None, None),
        P("row", "col", None, None),
        P("row", "col", None),
        P("row", "col", None),
        P("row", "col", None),
        P("row", "col", None),
        P("col", None),
        P(),
    )
    out_specs = (P("row", "col", None, None), P("row", "col", None, None))
    return jax.shard_map(body, mesh=mesh, in_specs=in_specs, out_specs=out_specs, check_vma=False)
```

profile of v0, /device:TPU:0, one launch (start us, length us, event | category | flops | bytes accessed | tf_op | source)
XLA Modules:
  0.0 438.9 jit_solution(14853244521627657069)
XLA Ops:
  7.2 0.0 copy-start
  7.2 0.0 all-gather.6.cloned.1.call-start
  7.2 2.1 copy.31
  9.3 0.0 all-gather.6.cloned.1.call-update
  9.4 0.0 all-gather.14.cloned.1.call-start
  9.4 0.7 all-gather.14.cloned.1.call-update
  10.1 0.0 all-gather.10.cloned.1.call-start
  10.2 0.7 all-gather.10.cloned.1.call-update
  10.9 0.0 all-gather.8.cloned.1.call-start
  10.9 47.6 %all-gather.6.cloned.1.call-done = f32[2,2048,128]{1,2,0:T(8,128)} async-done(((f32[2,512,128]{1,2,0:T(8,128)}), f32[2,2048,128]{1,2,0:T(8,128)}) %all-gather.6.cloned.1.call-update) | async-done | bytes 2097168 | tf_op jit(solution)/shard_map/all_gather | solution.py:20
  58.5 6.2 %fusion.8 = f32[2,512,128]{1,2,0:T(8,128)S(1)} fusion(f32[2,2048,128]{1,2,0:T(8,128)} %all-gather.6.cloned.1.call-done, f32[512,2048]{1,0:T(8,128)} %param.14), kind=kOutput, calls=%fused_computation.14 | convolution fusion | flops 3221225472 | bytes 6815744 | tf_op jit(solution)/shard_map/ab,tbk->tak/dot_general | solution.py:17
  64.8 1.0 copy.32
  65.8 0.0 all-gather.8.cloned.1.call-update
  65.8 30.0 %all-gather.14.cloned.1.call-done = f32[16,512,128]{2,1,0:T(8,128)} async-done(((f32[2,512,128]{2,1,0:T(8,128)}), f32[16,512,128]{2,1,0:T(8,128)}) %all-gather.14.cloned.1.call-update) | async-done | bytes 4194320 | tf_op jit(solution)/shard_map/all_gather | solution.py:24
  95.9 4.8 %all-to-all-start = ((f32[16,512,128]{2,1,0:T(8,128)}), f32[16,512,128]{2,1,0:T(8,128)}, u32[]{:S(2)}, u32[]{:S(2)}) async-start(f32[16,512,128]{2,1,0:T(8,128)} %all-gather.14.cloned.1.call-done), calls=%async_computation.1 | async-start | bytes 8388608 | tf_op jit(solution)/shard_map/all_to_all | solution.py:28
  100.7 0.0 all-gather.12.cloned.1.call-start
  100.8 0.5 all-gather.12.cloned.1.call-update
  101.3 0.2 reduce-scatter.2.cloned.1.call-start
  101.5 52.2 %all-gather.10.cloned.1.call-done = f32[1,2048,128]{2,1,0:T(8,128)} async-done(((f32[1,512,128]{2,1,0:T(8,128)}), f32[1,2048,128]{2,1,0:T(8,128)}) %all-gather.10.cloned.1.call-update) | async-done | bytes 1048592 | tf_op jit(solution)/shard_map/all_gather | solution.py:14
  153.7 7.0 %convolution_bitcast_fusion.1 = f32[512,128,1]{0,1,2:T(8,128)S(1)} fusion(f32[512,2048]{1,0:T(8,128)} %param.14, f32[1,2048,128]{2,1,0:T(8,128)} %all-gather.10.cloned.1.call-done), kind=kOutput, calls=%fused_computation.15 | convolution fusion | flops 1610612736 | bytes 5505024 | tf_op jit(solution)/shard_map/ab,tbk->tak/dot_general | solution.py:11
  160.7 30.1 %all-gather.8.cloned.1.call-done = f32[16,512,128]{2,1,0:T(8,128)} async-done(((f32[2,512,128]{2,1,0:T(8,128)}), f32[16,512,128]{2,1,0:T(8,128)}) %all-gather.8.cloned.1.call-update) | async-done | bytes 4194320 | tf_op jit(solution)/shard_map/all_gather | solution.py:25
  190.7 9.8 %convolution_bitcast_fusion = f32[1,16,128,128]{2,3,1,0:T(8,128)} fusion(f32[16,512,128]{2,1,0:T(8,128)} %all-gather.8.cloned.1.call-done, f32[512,128,1]{0,1,2:T(8,128)S(1)} %convolution_bitcast_fusion.1), kind=kOutput, calls=%fused_computation.13 | convolution fusion | flops 1610612736 | bytes 5505024 | tf_op jit(solution)/shard_map/iak,jal->ijkl/dot_general | solution.py:29
  200.6 0.0 reduce-scatter.2.cloned.1.call-update
  200.6 5.7 %copy.35 = f32[1,4,2048,128]{2,3,1,0:T(8,128)} copy(f32[1,4,2048,128]{3,2,1,0:T(8,128)} %param.8) | data formatting | bytes 8388608 | tf_op args[0]
  206.3 5.4 %copy.37 = f32[1,4,2048,128]{2,3,1,0:T(8,128)} copy(f32[1,4,2048,128]{3,2,1,0:T(8,128)} %param.9) | data formatting | bytes 8388608 | tf_op args[1]
  211.8 16.7 %all-gather.12.cloned.1.call-done = f32[1,2048,128]{2,1,0:T(8,128)} async-done(((f32[1,512,128]{2,1,0:T(8,128)}), f32[1,2048,128]{2,1,0:T(8,128)}) %all-gather.12.cloned.1.call-update) | async-done | bytes 1048592 | tf_op jit(solution)/shard_map/all_gather | solution.py:27
  228.5 28.2 %reduce-scatter.2.cloned.1.call-done = f32[1,4,128,128]{2,3,1,0:T(8,128)} async-done(((f32[1,16,128,128]{2,3,1,0:T(8,128)}), f32[1,4,128,128]{2,3,1,0:T(8,128)}) %reduce-scatter.2.cloned.1.call-update) | async-done | bytes 262160 | tf_op jit(solution)/shard_map/reduce_scatter | solution.py:30
  256.7 6.7 %negate_bitcast_fusion = f32[1,4,2048,128]{2,3,1,0:T(8,128)} fusion(f32[1,2048,128]{2,1,0:T(8,128)} %all-gather.12.cloned.1.call-done, f32[1,4,128,128]{2,3,1,0:T(8,128)} %reduce-scatter.2.cloned.1.call-done), kind=kOutput, calls=%fused_computation.12 | convolution fusion | flops 1611661312 | bytes 5505024 | tf_op jit(solution)/shard_map/iak,ijkl->ijal/dot_general | solution.py:31
  263.4 0.0 all-to-all-done
  263.4 5.4 %copy.36 = f32[4,4,512,128]{2,0,3,1:T(4,128)} copy(f32[4,4,512,128]{3,2,1,0:T(8,128)} %bitcast.15) | data formatting | bytes 8388608 | tf_op jit(solution)/shard_map/all_to_all | solution.py:28
  268.9 6.0 %broadcast_in_dim.9 = f32[1,4,2048,128]{2,3,1,0:T(8,128)} reshape(f32[4,4,512,128]{2,1,3,0:T(4,128)} %bitcast.83) | data formatting | bytes 8388608 | tf_op jit(solution)/shard_map/broadcast_in_dim | solution.py:33
  274.9 9.7 %fusion.1 = f32[4,256,128]{2,1,0:T(8,128)S(1)} fusion(f32[1,4,2048,128]{2,3,1,0:T(8,128)} %broadcast_in_dim.9, f32[1,4,2048,128]{2,3,1,0:T(8,128)} %copy.37, f32[2048,128]{1,0:T(8,128)S(1)} %copy-done), kind=kOutput, calls=%fused_computation.3 | convolution fusion | flops 3223322624 | bytes 9961472 | tf_op jit(solution)/shard_map/ijar,ak->ijrk/dot_general | solution.py:34
  284.7 14.0 %fusion.3 = f32[4,2048,128]{2,1,0:T(8,128)S(1)} fusion(f32[4,256,128]{2,1,0:T(8,128)S(1)} %fusion.1, f32[1,4,2048,128]{2,3,1,0:T(8,128)S(1)} %copy-done.5, f32[1,4,2048,128]{2,3,1,0:T(8,128)S(1)} %copy-done.3), kind=kOutput, calls=%fused_computation.5 | convolution fusion | flops 3223322624 | bytes 13107200 | tf_op jit(solution)/shard_map/ijar,ijrk->ijak/dot_general | solution.py:35
  298.7 0.0 copy-start.2
  298.7 6.9 %fusion.21 = f32[4,128,128]{1,2,0:T(8,128)S(1)} fusion(f32[4,2048,128]{2,1,0:T(8,128)S(1)} %fusion.3), kind=kOutput, calls=%fused_computation.32 | convolution fusion | flops 1610612736 | bytes 4456448 | tf_op jit(solution)/shard_map/ijak,ijal->ijkl/dot_general | solution.py:36
  305.7 0.1 copy.41
  305.9 47.1 %custom-call.8 = f32[1,4,128,128]{3,2,1,0:T(8,128)S(1)} custom-call(f32[1,4,128,128]{3,2,1,0:T(8,128)S(1)} %fusion.14), custom_call_target="Cholesky" | custom-call | tf_op jit(solution)/shard_map/jit(cholesky)/cholesky | solution.py:37
  353.0 0.1 compare_reduce_fusion
  353.1 0.1 select_bitcast_fusion
  353.3 39.3 %custom-call.9 = f32[4,1,128,128]{2,3,1,0:T(8,128)S(1)} custom-call(f32[4,1,128,128]{3,2,1,0:T(8,128)S(1)} %select_bitcast_fusion), custom_call_target="InvertDiagBlocksLowerTriangular" | custom-call | tf_op jit(solution)/shard_map/jit(_solve_triangular)/vmap()/triangular_solve | solution.py:38
  392.6 5.9 %fusion.4 = f32[4,128,2048]{2,1,0:T(8,128)S(1)} fusion(f32[4,2048,128]{2,1,0:T(8,128)} %copy-done.2, f32[4,1,128,128]{2,3,1,0:T(8,128)S(1)} %custom-call.9), kind=kOutput, calls=%fused_computation.6 | convolution fusion | flops 1610612736 | bytes 8650752 | tf_op jit(solution)/shard_map/jit(_solve_triangular)/vmap()/triangular_solve | solution.py:38
  398.5 7.4 %fusion.2 = f32[4,256,128]{2,1,0:T(8,128)S(1)} fusion(f32[4,128,2048]{2,1,0:T(8,128)S(1)} %fusion.4, f32[1,4,2048,128]{2,3,1,0:T(8,128)S(1)} %copy-done.6, f32[1,4,2048,128]{2,3,1,0:T(8,128)S(1)} %copy-done.4), kind=kOutput, calls=%fused_computation.4 | convolution fusion | flops 3223322624 | bytes 13107200 | tf_op jit(solution)/shard_map/ijar,ijak->ijrk/dot_general | solution.py:40
  405.9 0.0 copy-start.8
  405.9 2.5 multiply_bitcast_fusion.1
  408.5 1.1 copy-done.7
  409.6 1.3 copy-done.8
  410.9 15.5 %multiply_bitcast_fusion = f32[1,4,2048,128]{3,2,1,0:T(8,128)} fusion(f32[4,256,128]{2,1,0:T(8,128)S(1)} %fusion.2, f32[1,4,2048,128]{2,3,1,0:T(8,128)S(1)} %copy-done.8, f32[1,4,2048,128]{2,3,1,0:T(8,128)S(1)} %copy-done.7), kind=kOutput, calls=%fused_computation.10 | convolution fusion | flops 3224371200 | bytes 13107200 | tf_op jit(solution)/shard_map/ijar,ijrk->ijak/dot_general | solution.py:42
  426.4 5.3 %copy.45 = f32[1,4,2048,128]{3,2,1,0:T(8,128)} copy(f32[1,4,2048,128]{2,3,1,0:T(8,128)} %multiply_bitcast_fusion.1) | data formatting | bytes 8388608
  (17 shorter events, 0.1 us)
Async XLA Ops:
  7.2 267.7 %copy-start = (f32[2048,128]{1,0:T(8,128)S(1)}, f32[2048,128]{1,0:T(8,128)}, u32[]{:S(2)}) copy-start(f32[2048,128]{1,0:T(8,128)} %param.15) | copy-start | bytes 3145732
  7.2 51.4 %all-gather.6.cloned.1.call-start = ((), (), s32[]{:S(2)}) async-start(), calls=%async_computation.2 | async-start | bytes 2621440 | tf_op jit(solution)/shard_map/all_gather | solution.py:20
  9.4 86.5 %all-gather.14.cloned.1.call-start = ((), (), s32[]{:S(2)}) async-start(), calls=%async_computation.7 | async-start | bytes 4718592 | tf_op jit(solution)/shard_map/all_gather | solution.py:24
  10.1 143.6 %all-gather.10.cloned.1.call-start = ((), (), s32[]{:S(2)}) async-start(), calls=%async_computation.4 | async-start | bytes 1310720 | tf_op jit(solution)/shard_map/all_gather | solution.py:14
  10.9 179.9 %all-gather.8.cloned.1.call-start = ((), (), s32[]{:S(2)}) async-start(), calls=%async_computation.3 | async-start | bytes 4718592 | tf_op jit(solution)/shard_map/all_gather | solution.py:25
  95.9 167.6 %all-to-all-start = ((f32[16,512,128]{2,1,0:T(8,128)}), f32[16,512,128]{2,1,0:T(8,128)}, u32[]{:S(2)}, u32[]{:S(2)}) async-start(f32[16,512,128]{2,1,0:T(8,128)} %all-gather.14.cloned.1.call-done), calls=%async_computation.1 | async-start | bytes 8388608 | tf_op jit(solution)/shard_map/all_to_all | solution.py:28
  100.7 127.8 %all-gather.12.cloned.1.call-start = ((), (), s32[]{:S(2)}) async-start(), calls=%async_computation.6 | async-start | bytes 1310720 | tf_op jit(solution)/shard_map/all_gather | solution.py:27
  101.3 155.4 %reduce-scatter.2.cloned.1.call-start = ((), (), s32[]{:S(2)}) async-start(), calls=%async_computation.5 | async-start | bytes 1310720 | tf_op jit(solution)/shard_map/reduce_scatter | solution.py:30
  274.9 9.7 %copy-start.3 = (f32[1,4,2048,128]{2,3,1,0:T(8,128)S(1)}, f32[1,4,2048,128]{2,3,1,0:T(8,128)}, u32[]{:S(2)}) copy-start(f32[1,4,2048,128]{2,3,1,0:T(8,128)} %copy.35) | copy-start | bytes 12582916
  274.9 9.7 %copy-start.5 = (f32[1,4,2048,128]{2,3,1,0:T(8,128)S(1)}, f32[1,4,2048,128]{2,3,1,0:T(8,128)}, u32[]{:S(2)}) copy-start(f32[1,4,2048,128]{2,3,1,0:T(8,128)} %negate_bitcast_fusion) | copy-start | bytes 12582916
  298.7 7.0 %copy-start.2 = (f32[4,2048,128]{2,1,0:T(8,128)}, f32[4,2048,128]{2,1,0:T(8,128)S(1)}, u32[]{:S(2)}) copy-start(f32[4,2048,128]{2,1,0:T(8,128)S(1)} %fusion.3) | copy-start | bytes 12582916
  392.6 5.9 %copy-start.4 = (f32[1,4,2048,128]{2,3,1,0:T(8,128)S(1)}, f32[1,4,2048,128]{2,3,1,0:T(8,128)}, u32[]{:S(2)}) copy-start(f32[1,4,2048,128]{2,3,1,0:T(8,128)} %copy.35) | copy-start | bytes 12582916
  392.6 5.9 %copy-start.6 = (f32[1,4,2048,128]{2,3,1,0:T(8,128)S(1)}, f32[1,4,2048,128]{2,3,1,0:T(8,128)}, u32[]{:S(2)}) copy-start(f32[1,4,2048,128]{2,3,1,0:T(8,128)} %negate_bitcast_fusion) | copy-start | bytes 12582916
  405.9 3.7 copy-start.7
  405.9 5.0 %copy-start.8 = (f32[1,4,2048,128]{2,3,1,0:T(8,128)S(1)}, f32[1,4,2048,128]{2,3,1,0:T(8,128)}, u32[]{:S(2)}) copy-start(f32[1,4,2048,128]{2,3,1,0:T(8,128)} %broadcast_in_dim.9) | copy-start | bytes 12582916
  410.9 20.9 %copy-start.1 = (f32[2048,128]{1,0:T(8,128)S(1)}, f32[2048,128]{1,0:T(8,128)}, u32[]{:S(2)}) copy-start(f32[2048,128]{1,0:T(8,128)} %param.15) | copy-start | bytes 3145732
Sparse Core Ops, SparseCore 0:
  10.1 48.3 all-gather.5
  60.4 35.3 all-gather.13
  97.4 56.2 all-gather.9
  156.0 34.6 all-gather.7
  192.1 36.3 all-gather.11
  231.2 25.4 reduce-scatter.1
where the time goes:
time: 442 us; the launch traced here: 439 us
  waiting for transfers between devices  207 us (47%)
  other arithmetic  89.3 us (20%)
  matrix products  89.2 us (20%)
  local copies, waits for them, and re-layouts  33.7 us (8%)
  between operations  14.6 us (3%)
  starting transfers between devices  5.25 us (1%)
    all_gather x1, waiting for transfers between devices, body(): lax.all_gather(row_panel_v, 'col', axis=1, tiled=True)  52.2 us
    all_gather x1, waiting for transfers between devices, body(): lax.all_gather(col_panel_v, 'col', axis=1, tiled=True)  47.6 us
    another operation x4, other arithmetic, body(): factor = jnp.linalg.cholesky(gram_matrix)  47.3 us
    another operation x3, other arithmetic, body(): jax.scipy.linalg.solve_triangular(factor, jnp.swapaxes(sample, -1, -2), l...  39.4 us
    all_gather x1, waiting for transfers between devices, body(): lax.all_gather(second, 'row', axis=0, tiled=True)  30.1 us
    all_gather x1, waiting for transfers between devices, body(): lax.all_gather(col_panel_u, 'row', axis=0, tiled=True)  30 us
    reduce_scatter x1, waiting for transfers between devices, body(): lax.psum_scatter(partial_cores, 'col', scatter_dimension=1, tiled=True)  28.2 us
    unnamed x22, local copies, waits for them, and re-layouts  21 us
  transfers between devices with their start and end apart: 7, of which 6 were waited for; matrix products, arithmetic and copies ran while one was open for 10% of the time, Pallas kernels for 0%

commit v1 on v0

--- a/solution.py
+++ b/solution.py
@@ -7,6 +7,22 @@
 highest = lax.Precision.HIGHEST
 
 
+def summed_both_ways(shard, axis, dim, product):
+    size, index, extent = (lax.axis_size(axis), lax.axis_index(axis), shard.shape[dim])
+    forward = [(i, (i + 1) % size) for i in range(size)]
+    behind = [(i, (i - 1) % size) for i in range(size)]
+    half = size // 2
+    from_left = from_right = shard
+    total = product(shard, index * extent)
+    for lap in range(1, half + 1):
+        from_left = lax.ppermute(from_left, axis, forward)
+        if lap < size - half:
+            from_right = lax.ppermute(from_right, axis, behind)
+            total = total + product(from_right, (index + lap) % size * extent)
+        total = total + product(from_left, (index - lap) % size * extent)
+    return total
+
+
 def body(tile_u, tile_v, row_panel_u, row_panel_v, col_panel_u, col_panel_v, diag_inverse, sketch):
     first = jnp.einsum(
         "ab,tbk->tak",
@@ -14,11 +30,16 @@
         lax.all_gather(row_panel_v, "col", axis=1, tiled=True),
         precision=highest,
     )
-    second = jnp.einsum(
-        "ab,tbk->tak",
-        diag_inverse,
-        lax.all_gather(col_panel_v, "col", axis=1, tiled=True),
-        precision=highest,
+    second = summed_both_ways(
+        col_panel_v,
+        "col",
+        1,
+        lambda shard, offset: jnp.einsum(
+            "ab,tbk->tak",
+            lax.dynamic_slice_in_dim(diag_inverse, offset, shard.shape[1], axis=1),
+            shard,
+            precision=highest,
+        ),
     )
     col_u_rows, col_v_rows = (
         lax.all_gather(col_panel_u, "row", axis=0, tiled=True),

time: 442 us -> 396 us (0.90)
  waiting for transfers between devices: 207 us -> 157 us
  starting transfers between devices: 5.25 us -> 10.5 us
    all_gather x1 -> x0, waiting for transfers between devices: 47.6 us -> none  [body(): lax.all_gather(col_panel_v, 'col', axis=1, tiled=True)]
    all_gather x1, waiting for transfers between devices: 30 us -> 0.02 us  [body(): lax.all_gather(col_panel_u, 'row', axis=0, tiled=True)]
    ppermute x0 -> x3, waiting for transfers between devices: none -> 28.8 us  [the longest x2 18.8 us: summed_both_ways(): from_left = lax.ppermute(from_left, axis, forward)]
    ppermute x0 -> x3, starting transfers between devices: none -> 5.2 us  [the longest x2 3.11 us: summed_both_ways(): from_left = lax.ppermute(from_left, axis, forward)]
    unnamed x22 -> x23, local copies, waits for them, and re-layouts: 21 us -> 19.2 us
  transfers between devices with their start and end apart: 7 -> 9, of which waited for: 6 -> 7; matrix products, arithmetic and copies ran while one was open for 10% -> 11% of each run, Pallas kernels for 0% -> 0%
where the time goes in v1:
time: 396 us; the launch traced here: 392 us
  waiting for transfers between devices  157 us (40%)
  matrix products  90.4 us (23%)
  other arithmetic  89.3 us (23%)
  local copies, waits for them, and re-layouts  30.8 us (8%)
  between operations  14.2 us (4%)
  starting transfers between devices  10.5 us (3%)
    all_gather x1, waiting for transfers between devices, body(): lax.all_gather(row_panel_v, 'col', axis=1, tiled=True)  51 us
    another operation x4, other arithmetic, body(): factor = jnp.linalg.cholesky(gram_matrix)  47.3 us
    another operation x3, other arithmetic, body(): jax.scipy.linalg.solve_triangular(factor, jnp.swapaxes(sample, -1, -2), l...  39.4 us
    all_gather x1, waiting for transfers between devices, body(): lax.all_gather(second, 'row', axis=0, tiled=True)  29.4 us
    reduce_scatter x1, waiting for transfers between devices, body(): lax.psum_scatter(partial_cores, 'col', scatter_dimension=1, tiled=True)  28.7 us
    unnamed x23, local copies, waits for them, and re-layouts  19.2 us
    ppermute x2, waiting for transfers between devices, summed_both_ways(): from_left = lax.ppermute(from_left, axis, forward)  18.8 us
    all_gather x1, waiting for transfers between devices, body(): row_u_full = lax.all_gather(row_panel_u, 'col', axis=1, tiled=True)  16.7 us
  transfers between devices with their start and end apart: 9, of which 7 were waited for; matrix products, arithmetic and copies ran while one was open for 11% of the time, Pallas kernels for 0%

profile of v1, /device:TPU:0, one launch (start us, length us, event | category | flops | bytes accessed | tf_op | source)
XLA Modules:
  0.0 391.8 jit_solution(15450349545018930019)
XLA Ops:
  7.2 0.0 copy-start
  7.2 0.0 all-gather.11.cloned.1.call-start
  7.2 0.7 all-gather.11.cloned.1.call-update
  7.9 0.0 all-gather.7.cloned.1.call-start
  8.0 0.7 all-gather.7.cloned.1.call-update
  8.7 0.0 all-gather.5.cloned.1.call-start
  8.7 3.1 collective-permute-start.1
  11.8 2.1 collective-permute-start
  13.9 2.5 fusion.13
  16.4 10.5 %collective-permute-done.1 = f32[2,512,128]{2,1,0:T(8,128)S(1)} collective-permute-done((f32[2,512,128]{2,1,0:T(8,128)}, f32[2,512,128]{2,1,0:T(8,128)S(1)}, u32[]{:S(2)}, u32[]{:S(2)}) %collective-permute-start.1) | collective-permute-done | bytes 524320 | tf_op jit(solution)/shard_map/ppermute | solution.py:18
  26.9 10.0 %collective-permute-done = f32[2,512,128]{2,1,0:T(8,128)S(1)} collective-permute-done((f32[2,512,128]{2,1,0:T(8,128)}, f32[2,512,128]{2,1,0:T(8,128)S(1)}, u32[]{:S(2)}, u32[]{:S(2)}) %collective-permute-start) | collective-permute-done | bytes 524320 | tf_op jit(solution)/shard_map/ppermute | solution.py:20
  36.9 2.2 convolution_add_fusion.2
  39.1 1.0 convolution_add_fusion.1
  40.1 8.4 %collective-permute-done.2 = f32[2,512,128]{2,1,0:T(8,128)S(1)} collective-permute-done((f32[2,512,128]{2,1,0:T(8,128)S(1)}, f32[2,512,128]{2,1,0:T(8,128)S(1)}, u32[]{:S(2)}, u32[]{:S(2)}) %collective-permute-start.2) | collective-permute-done | bytes 524320 | tf_op jit(solution)/shard_map/ppermute | solution.py:18
  48.5 1.8 fusion.6
  50.3 0.0 all-gather.5.cloned.1.call-update
  50.3 0.0 all-gather.11.cloned.1.call-done
  50.3 4.9 %all-to-all-start = ((f32[16,512,128]{2,1,0:T(8,128)}), f32[16,512,128]{2,1,0:T(8,128)}, u32[]{:S(2)}, u32[]{:S(2)}) async-start(f32[16,512,128]{2,1,0:T(8,128)} %all-gather.11.cloned.1.call-done), calls=%async_computation.1 | async-start | bytes 8388608 | tf_op jit(solution)/shard_map/all_to_all | solution.py:49
  55.2 0.0 all-gather.9.cloned.1.call-start
  55.2 0.5 all-gather.9.cloned.1.call-update
  55.8 0.3 reduce-scatter.2.cloned.1.call-start
  56.1 51.0 %all-gather.7.cloned.1.call-done = f32[1,2048,128]{2,1,0:T(8,128)} async-done(((f32[1,512,128]{2,1,0:T(8,128)}), f32[1,2048,128]{2,1,0:T(8,128)}) %all-gather.7.cloned.1.call-update) | async-done | bytes 1048592 | tf_op jit(solution)/shard_map/all_gather | solution.py:30
  107.1 7.0 %convolution_bitcast_fusion.1 = f32[512,128,1]{0,1,2:T(8,128)S(1)} fusion(f32[512,2048]{1,0:T(8,128)} %param.14, f32[1,2048,128]{2,1,0:T(8,128)} %all-gather.7.cloned.1.call-done), kind=kOutput, calls=%fused_computation.16 | convolution fusion | flops 1610612736 | bytes 5505024 | tf_op jit(solution)/shard_map/ab,tbk->tak/dot_general | solution.py:27
  114.0 29.4 %all-gather.5.cloned.1.call-done = f32[16,512,128]{2,1,0:T(8,128)} async-done(((f32[2,512,128]{2,1,0:T(8,128)}), f32[16,512,128]{2,1,0:T(8,128)}) %all-gather.5.cloned.1.call-update) | async-done | bytes 4194320 | tf_op jit(solution)/shard_map/all_gather | solution.py:46
  143.4 9.8 %convolution_bitcast_fusion = f32[1,16,128,128]{2,3,1,0:T(8,128)} fusion(f32[16,512,128]{2,1,0:T(8,128)} %all-gather.5.cloned.1.call-done, f32[512,128,1]{0,1,2:T(8,128)S(1)} %convolution_bitcast_fusion.1), kind=kOutput, calls=%fused_computation.11 | convolution fusion | flops 1610612736 | bytes 5505024 | tf_op jit(solution)/shard_map/iak,jal->ijkl/dot_general | solution.py:50
  153.2 0.0 reduce-scatter.2.cloned.1.call-update
  153.2 5.9 %copy.33 = f32[1,4,2048,128]{2,3,1,0:T(8,128)} copy(f32[1,4,2048,128]{3,2,1,0:T(8,128)} %param.8) | data formatting | bytes 8388608 | tf_op args[0]
  159.2 5.5 %copy.35 = f32[1,4,2048,128]{2,3,1,0:T(8,128)} copy(f32[1,4,2048,128]{3,2,1,0:T(8,128)} %param.9) | data formatting | bytes 8388608 | tf_op args[1]
  164.7 16.7 %all-gather.9.cloned.1.call-done = f32[1,2048,128]{2,1,0:T(8,128)} async-done(((f32[1,512,128]{2,1,0:T(8,128)}), f32[1,2048,128]{2,1,0:T(8,128)}) %all-gather.9.cloned.1.call-update) | async-done | bytes 1048592 | tf_op jit(solution)/shard_map/all_gather | solution.py:48
  181.4 28.7 %reduce-scatter.2.cloned.1.call-done = f32[1,4,128,128]{2,3,1,0:T(8,128)} async-done(((f32[1,16,128,128]{2,3,1,0:T(8,128)}), f32[1,4,128,128]{2,3,1,0:T(8,128)}) %reduce-scatter.2.cloned.1.call-update) | async-done | bytes 262160 | tf_op jit(solution)/shard_map/reduce_scatter | solution.py:51
  210.1 6.7 %negate_bitcast_fusion = f32[1,4,2048,128]{2,3,1,0:T(8,128)} fusion(f32[1,2048,128]{2,1,0:T(8,128)} %all-gather.9.cloned.1.call-done, f32[1,4,128,128]{2,3,1,0:T(8,128)} %reduce-scatter.2.cloned.1.call-done), kind=kOutput, calls=%fused_computation.10 | convolution fusion | flops 1611661312 | bytes 5505024 | tf_op jit(solution)/shard_map/iak,ijkl->ijal/dot_general | solution.py:52
  216.8 5.4 %copy.34 = f32[4,4,512,128]{2,0,3,1:T(4,128)} copy(f32[4,4,512,128]{3,2,1,0:T(8,128)} %bitcast.18) | data formatting | bytes 8388608 | tf_op jit(solution)/shard_map/all_to_all | solution.py:49
  222.2 6.0 %broadcast_in_dim.9 = f32[1,4,2048,128]{2,3,1,0:T(8,128)} reshape(f32[4,4,512,128]{2,1,3,0:T(4,128)} %bitcast.93) | data formatting | bytes 8388608 | tf_op jit(solution)/shard_map/broadcast_in_dim | solution.py:54
  228.3 9.5 %fusion.1 = f32[4,256,128]{2,1,0:T(8,128)S(1)} fusion(f32[1,4,2048,128]{2,3,1,0:T(8,128)} %broadcast_in_dim.9, f32[1,4,2048,128]{2,3,1,0:T(8,128)} %copy.35, f32[2048,128]{1,0:T(8,128)S(1)} %copy-done), kind=kOutput, calls=%fused_computation.3 | convolution fusion | flops 3223322624 | bytes 9961472 | tf_op jit(solution)/shard_map/ijar,ak->ijrk/dot_general | solution.py:55
  237.8 14.1 %fusion.3 = f32[4,2048,128]{2,1,0:T(8,128)S(1)} fusion(f32[4,256,128]{2,1,0:T(8,128)S(1)} %fusion.1, f32[1,4,2048,128]{2,3,1,0:T(8,128)S(1)} %copy-done.5, f32[1,4,2048,128]{2,3,1,0:T(8,128)S(1)} %copy-done.3), kind=kOutput, calls=%fused_computation.5 | convolution fusion | flops 3223322624 | bytes 13107200 | tf_op jit(solution)/shard_map/ijar,ijrk->ijak/dot_general | solution.py:56
  251.9 6.9 %fusion.30 = f32[4,128,128]{1,2,0:T(8,128)S(1)} fusion(f32[4,2048,128]{2,1,0:T(8,128)S(1)} %fusion.3), kind=kOutput, calls=%fused_computation.46 | convolution fusion | flops 1610612736 | bytes 4456448 | tf_op jit(solution)/shard_map/ijak,ijal->ijkl/dot_general | solution.py:57
  258.9 0.1 copy.39
  259.0 47.1 %custom-call.8 = f32[1,4,128,128]{3,2,1,0:T(8,128)S(1)} custom-call(f32[1,4,128,128]{3,2,1,0:T(8,128)S(1)} %fusion.19), custom_call_target="Cholesky" | custom-call | tf_op jit(solution)/shard_map/jit(cholesky)/cholesky | solution.py:58
  306.2 0.1 compare_reduce_fusion
  306.3 0.1 select_bitcast_fusion
  306.5 39.3 %custom-call.9 = f32[4,1,128,128]{2,3,1,0:T(8,128)S(1)} custom-call(f32[4,1,128,128]{3,2,1,0:T(8,128)S(1)} %select_bitcast_fusion), custom_call_target="InvertDiagBlocksLowerTriangular" | custom-call | tf_op jit(solution)/shard_map/jit(_solve_triangular)/vmap()/triangular_solve | solution.py:59
  345.8 6.1 %fusion.4 = f32[4,128,2048]{2,1,0:T(8,128)S(1)} fusion(f32[4,2048,128]{2,1,0:T(8,128)} %copy-done.2, f32[4,1,128,128]{2,3,1,0:T(8,128)S(1)} %custom-call.9), kind=kOutput, calls=%fused_computation.6 | convolution fusion | flops 1610612736 | bytes 8650752 | tf_op jit(solution)/shard_map/jit(_solve_triangular)/vmap()/triangular_solve | solution.py:59
  351.9 7.4 %fusion.2 = f32[4,256,128]{2,1,0:T(8,128)S(1)} fusion(f32[4,128,2048]{2,1,0:T(8,128)S(1)} %fusion.4, f32[1,4,2048,128]{2,3,1,0:T(8,128)S(1)} %copy-done.6, f32[1,4,2048,128]{2,3,1,0:T(8,128)S(1)} %copy-done.4), kind=kOutput, calls=%fused_computation.4 | convolution fusion | flops 3223322624 | bytes 13107200 | tf_op jit(solution)/shard_map/ijar,ijak->ijrk/dot_general | solution.py:61
  359.3 2.5 multiply_bitcast_fusion.1
  361.9 1.1 copy-done.7
  363.0 1.3 copy-done.8
  364.3 15.4 %multiply_bitcast_fusion = f32[1,4,2048,128]{3,2,1,0:T(8,128)} fusion(f32[4,256,128]{2,1,0:T(8,128)S(1)} %fusion.2, f32[1,4,2048,128]{2,3,1,0:T(8,128)S(1)} %copy-done.8, f32[1,4,2048,128]{2,3,1,0:T(8,128)S(1)} %copy-done.7), kind=kOutput, calls=%fused_computation.8 | convolution fusion | flops 3224371200 | bytes 13107200 | tf_op jit(solution)/shard_map/ijar,ijrk->ijak/dot_general | solution.py:63
  379.7 5.3 %copy.43 = f32[1,4,2048,128]{3,2,1,0:T(8,128)} copy(f32[1,4,2048,128]{2,3,1,0:T(8,128)} %multiply_bitcast_fusion.1) | data formatting | bytes 8388608
  (23 shorter events, 0.1 us)
Async XLA Ops:
  7.2 221.1 %copy-start = (f32[2048,128]{1,0:T(8,128)S(1)}, f32[2048,128]{1,0:T(8,128)}, u32[]{:S(2)}) copy-start(f32[2048,128]{1,0:T(8,128)} %param.15) | copy-start | bytes 3145732
  7.2 43.1 %all-gather.11.cloned.1.call-start = ((), (), s32[]{:S(2)}) async-start(), calls=%async_computation.6 | async-start | bytes 4718592 | tf_op jit(solution)/shard_map/all_gather | solution.py:45
  7.9 99.1 %all-gather.7.cloned.1.call-start = ((), (), s32[]{:S(2)}) async-start(), calls=%async_computation.3 | async-start | bytes 1310720 | tf_op jit(solution)/shard_map/all_gather | solution.py:30
  8.7 134.7 %all-gather.5.cloned.1.call-start = ((), (), s32[]{:S(2)}) async-start(), calls=%async_computation.2 | async-start | bytes 4718592 | tf_op jit(solution)/shard_map/all_gather | solution.py:46
  8.7 18.2 %collective-permute-start.1 = (f32[2,512,128]{2,1,0:T(8,128)}, f32[2,512,128]{2,1,0:T(8,128)S(1)}, u32[]{:S(2)}, u32[]{:S(2)}) collective-permute-start(f32[2,512,128]{2,1,0:T(8,128)} %param.13), channel_id=1, source_target_pairs={{0,1},{1,2},{2,3},{3,0},{4,5},{5,6},{6,7},{7,4},{8,9},{9,10},{10,1... | collective-permute-start | bytes 1572872 | tf_op jit(solution)/shard_map/ppermute | solution.py:18
  11.8 25.1 %collective-permute-start = (f32[2,512,128]{2,1,0:T(8,128)}, f32[2,512,128]{2,1,0:T(8,128)S(1)}, u32[]{:S(2)}, u32[]{:S(2)}) collective-permute-start(f32[2,512,128]{2,1,0:T(8,128)} %param.13), channel_id=1, source_target_pairs={{0,3},{1,0},{2,1},{3,2},{4,7},{5,4},{6,5},{7,6},{8,11},{9,8},{10,9... | collective-permute-start | bytes 1572872 | tf_op jit(solution)/shard_map/ppermute | solution.py:20
  13.9 25.2 %copy-start.9 = (f32[512,2048]{1,0:T(8,128)S(1)}, f32[512,2048]{1,0:T(8,128)}, u32[]{:S(2)}) copy-start(f32[512,2048]{1,0:T(8,128)} %param.14) | copy-start | bytes 12582916
  26.9 21.6 %collective-permute-start.2 = (f32[2,512,128]{2,1,0:T(8,128)S(1)}, f32[2,512,128]{2,1,0:T(8,128)S(1)}, u32[]{:S(2)}, u32[]{:S(2)}) collective-permute-start(f32[2,512,128]{2,1,0:T(8,128)S(1)} %collective-permute-done.1), channel_id=1, source_target_pairs={{0,1},{1,2},{2,3},{3,0},{4,5},{5,6},{6,7},{7,4},{8,9},{9,10},{10,1... | collective-permute-start | bytes 1572872 | tf_op jit(solution)/shard_map/ppermute | solution.py:18
  50.3 166.5 %all-to-all-start = ((f32[16,512,128]{2,1,0:T(8,128)}), f32[16,512,128]{2,1,0:T(8,128)}, u32[]{:S(2)}, u32[]{:S(2)}) async-start(f32[16,512,128]{2,1,0:T(8,128)} %all-gather.11.cloned.1.call-done), calls=%async_computation.1 | async-start | bytes 8388608 | tf_op jit(solution)/shard_map/all_to_all | solution.py:49
  55.2 126.2 %all-gather.9.cloned.1.call-start = ((), (), s32[]{:S(2)}) async-start(), calls=%async_computation.5 | async-start | bytes 1310720 | tf_op jit(solution)/shard_map/all_gather | solution.py:48
  55.8 154.3 %reduce-scatter.2.cloned.1.call-start = ((), (), s32[]{:S(2)}) async-start(), calls=%async_computation.4 | async-start | bytes 1310720 | tf_op jit(solution)/shard_map/reduce_scatter | solution.py:51
  228.3 9.5 %copy-start.3 = (f32[1,4,2048,128]{2,3,1,0:T(8,128)S(1)}, f32[1,4,2048,128]{2,3,1,0:T(8,128)}, u32[]{:S(2)}) copy-start(f32[1,4,2048,128]{2,3,1,0:T(8,128)} %copy.33) | copy-start | bytes 12582916
  228.3 9.5 %copy-start.5 = (f32[1,4,2048,128]{2,3,1,0:T(8,128)S(1)}, f32[1,4,2048,128]{2,3,1,0:T(8,128)}, u32[]{:S(2)}) copy-start(f32[1,4,2048,128]{2,3,1,0:T(8,128)} %negate_bitcast_fusion) | copy-start | bytes 12582916
  251.9 7.0 %copy-start.2 = (f32[4,2048,128]{2,1,0:T(8,128)}, f32[4,2048,128]{2,1,0:T(8,128)S(1)}, u32[]{:S(2)}) copy-start(f32[4,2048,128]{2,1,0:T(8,128)S(1)} %fusion.3) | copy-start | bytes 12582916
  345.8 6.1 %copy-start.4 = (f32[1,4,2048,128]{2,3,1,0:T(8,128)S(1)}, f32[1,4,2048,128]{2,3,1,0:T(8,128)}, u32[]{:S(2)}) copy-start(f32[1,4,2048,128]{2,3,1,0:T(8,128)} %copy.33) | copy-start | bytes 12582916
  345.8 6.1 %copy-start.6 = (f32[1,4,2048,128]{2,3,1,0:T(8,128)S(1)}, f32[1,4,2048,128]{2,3,1,0:T(8,128)}, u32[]{:S(2)}) copy-start(f32[1,4,2048,128]{2,3,1,0:T(8,128)} %negate_bitcast_fusion) | copy-start | bytes 12582916
  359.3 3.7 copy-start.7
  359.3 5.0 %copy-start.8 = (f32[1,4,2048,128]{2,3,1,0:T(8,128)S(1)}, f32[1,4,2048,128]{2,3,1,0:T(8,128)}, u32[]{:S(2)}) copy-start(f32[1,4,2048,128]{2,3,1,0:T(8,128)} %broadcast_in_dim.9) | copy-start | bytes 12582916
  364.3 20.7 %copy-start.1 = (f32[2048,128]{1,0:T(8,128)S(1)}, f32[2048,128]{1,0:T(8,128)}, u32[]{:S(2)}) copy-start(f32[2048,128]{1,0:T(8,128)} %param.15) | copy-start | bytes 3145732
Sparse Core Ops, SparseCore 0:
  9.9 39.2 all-gather.10
  50.8 56.2 all-gather.6
  109.5 33.8 all-gather.4
  144.8 36.5 all-gather.8
  184.1 25.9 reduce-scatter.1
